TPU v7x, 32 devices: a whole 2x2x4 slice. The times are simulated.
32 devices in a mesh: seq: 8 (over z, y), rep: 4 (over x, core).
Axes of the slice: x: 2, y: 2, z: 4, core: 2. Of those that a mesh axis runs over, the one named last changes fastest.
Arguments:
- head_out: bfloat16 [4, 4096, 4096], P('rep', 'seq'), may hold values from -6 to 6
- grad_out: bfloat16 [4, 4096, 3584], P('rep', 'seq'), may hold values from -6 to 6
- hash_codes: int32 [4, 16, 3584], P('rep'), may hold values from 0 to 511
- loss_mask: int32 [4096], P('seq'), may hold values 0 or 1
- query_ids: int32 [64], replicated, may hold values from 0 to 4095
Outputs:
- attribution: float32 [4096, 64], P(('seq', 'rep'))
All inputs are finite; a program needn't handle non-finite values. No bound on the sum of `loss_mask` on one device may be relied on, other than what follows from the above.
Results may differ from a plain program's by a relative error of at most 0.0025.
Values may be sent and summed in bfloat16 or wider, within the bound.
A program may use at most 64 MiB of HBM per device.

v0:
```python
import math
import jax
import jax.numpy as jnp
from jax import lax
from jax.sharding import PartitionSpec as P

ridge_shift = 0.25
norm_floor = 1e-06


def build_sketches(outputs, gradient, codes):
    head_count = codes.shape[0]
    sketch_width = outputs.shape[1] // head_count
    model_width = gradient.shape[1]
    sketch_scale = math.sqrt(sketch_width / model_width)
    columns = jnp.arange(sketch_width, dtype=jnp.int32)

    def one_head(head_index):
        head_codes = codes[head_index]
        bucket = head_codes % sketch_width
        sign_flip = 1 - 2 * (head_codes // sketch_width)
        count_table = jnp.where(bucket[:, None] == columns[None, :], sign_flip[:, None], 0).astype(
            jnp.bfloat16
        )
        counted = jnp.dot(gradient, count_table, preferred_element_type=jnp.float32)
        picked = lax.dynamic_slice_in_dim(
            outputs, head_index * sketch_width, sketch_width, 1
        ).astype(jnp.float32)
        return (picked * counted * sketch_scale).astype(jnp.bfloat16)

    return lax.map(one_head, jnp.arange(head_count, dtype=jnp.int32))


def solve_queries(gram_sum, chosen, token_count):
    sketch_width = gram_sum.shape[0]
    gram_sum = gram_sum / token_count + ridge_shift * jnp.eye(sketch_width, dtype=jnp.float32)
    factor = jnp.linalg.cholesky(gram_sum)
    return jax.scipy.linalg.cho_solve((factor, True), chosen.T).astype(jnp.bfloat16)


def on_device(head_out, grad_out, hash_codes, loss_mask, query_ids):
    sketches = build_sketches(head_out[0], grad_out[0], hash_codes[0])
    tok_rows = loss_mask.shape[0]
    out_rows = tok_rows // lax.axis_size("rep")
    mask_bf = loss_mask.astype(jnp.bfloat16)
    local_count = jnp.sum(loss_mask.astype(jnp.float32))
    token_count = lax.psum(local_count, "seq") + 1.0
    local_grams = jnp.einsum(
        "htk,htj->hkj",
        sketches * mask_bf[None, :, None],
        sketches,
        preferred_element_type=jnp.float32,
    )
    first_row = lax.axis_index("seq") * tok_rows
    query_hits = (
        query_ids[:, None] - first_row == jnp.arange(tok_rows, dtype=jnp.int32)[None, :]
    ).astype(jnp.bfloat16)
    local_chosen = jnp.einsum(
        "qt,htk->hqk", query_hits, sketches, preferred_element_type=jnp.float32
    )
    own_grams, own_chosen = (
        lax.psum_scatter(local_grams, "seq", scatter_dimension=0, tiled=True),
        lax.psum_scatter(local_chosen, "seq", scatter_dimension=0, tiled=True),
    )
    solved = jnp.stack(
        [
            solve_queries(own_grams[slot_index], own_chosen[slot_index], token_count)
            for slot_index in range(own_grams.shape[0])
        ]
    )
    solved_all = lax.all_gather(solved, "seq", axis=0, tiled=True)
    score_sum = jnp.einsum("htk,hkq->tq", sketches, solved_all, preferred_element_type=jnp.float32)
    contrib = lax.psum_scatter(score_sum, "rep", scatter_dimension=0, tiled=True)
    row_start = lax.axis_index("rep") * out_rows
    mask_rows = lax.dynamic_slice_in_dim(loss_mask, row_start, out_rows, 0).astype(jnp.float32)
    partial_value = jnp.sum(mask_rows[:, None] * contrib * contrib, 0)
    norm_sum = lax.psum(partial_value, ("seq", "rep")) / token_count
    return contrib / jnp.sqrt(norm_sum + norm_floor)


def solution(mesh):
    placed = (P("rep", "seq", None), P("rep", "seq", None), P("rep", None, None), P("seq"), P())
    return jax.shard_map(
        on_device, mesh=mesh, in_specs=placed, out_specs=P(("seq", "rep"), None), check_vma=False
    )
```

profile of v0, /device:TPU:0, one launch (start us, length us, event | category | flops | bytes accessed | tf_op | source)
XLA Modules:
  0.0 561.4 jit_solution(14292173351317738377)
XLA Ops:
  6.5 6.5 %copy.13 = bf16[1,512,4096]{1,2,0:T(8,128)(2,1)} copy(bf16[1,512,4096]{2,1,0:T(8,128)(2,1)} %param.10) | data formatting | bytes 8388608 | tf_op args[0]
  13.0 158.3 %while.17 = (s32[]{:T(128)}, bf16[16,512,256]{1,2,0:T(8,128)(2,1)}, s32[16]{0:T(128)S(1)}, bf16[512,4096]{0,1:T(8,128)(2,1)}, s32[16,3584]{1,0:T(8,128)}, /*inde...) while((s32[]{:T(128)}, bf16[16,512,256]{1,2,0:T(8,128)(2,1)}, ...), condition=%wide.region_1.2_spmd.clone, body=%wide.region_0.1_spmd.clone.sunk | while | flops 942876160 | bytes 4295377 | solution.py:31
  15.8 0.9 dynamic-slice_reduce_fusion.2
  16.8 6.1 %fusion.76 = bf16[16,512,256]{1,2,0:T(8,128)(2,1)} fusion(bf16[16,512,256]{1,2,0:T(8,128)(2,1)} %get-tuple-element.293, s32[]{:T(128)} %get-tuple-element.292, bf16[512,3584]{1,0:T(8,128)(2,1)} %get-tuple-element.308, s32[3584]{0:T(1024)S(1)} %get-tuple-element.267, s32[3584]{0:T(1024)S(1)} %get-tuple-element.268, ...), kind=kOutput, calls=%fused_computation.16.clone.1 | convolution fusion | flops 942800896 | bytes 4223492 | tf_op jit(solution)/shard_map/while/body/eval_jaxpr/dot_general | solution.py:25
  25.7 0.9 dynamic-slice_reduce_fusion.2
  26.7 6.1 %fusion.76 = bf16[16,512,256]{1,2,0:T(8,128)(2,1)} fusion(bf16[16,512,256]{1,2,0:T(8,128)(2,1)} %get-tuple-element.293, s32[]{:T(128)} %get-tuple-element.292, bf16[512,3584]{1,0:T(8,128)(2,1)} %get-tuple-element.308, s32[3584]{0:T(1024)S(1)} %get-tuple-element.267, s32[3584]{0:T(1024)S(1)} %get-tuple-element.268, ...), kind=kOutput, calls=%fused_computation.16.clone.1 | convolution fusion | flops 942800896 | bytes 4223492 | tf_op jit(solution)/shard_map/while/body/eval_jaxpr/dot_general | solution.py:25
  35.6 0.9 dynamic-slice_reduce_fusion.2
  36.6 6.1 %fusion.76 = bf16[16,512,256]{1,2,0:T(8,128)(2,1)} fusion(bf16[16,512,256]{1,2,0:T(8,128)(2,1)} %get-tuple-element.293, s32[]{:T(128)} %get-tuple-element.292, bf16[512,3584]{1,0:T(8,128)(2,1)} %get-tuple-element.308, s32[3584]{0:T(1024)S(1)} %get-tuple-element.267, s32[3584]{0:T(1024)S(1)} %get-tuple-element.268, ...), kind=kOutput, calls=%fused_computation.16.clone.1 | convolution fusion | flops 942800896 | bytes 4223492 | tf_op jit(solution)/shard_map/while/body/eval_jaxpr/dot_general | solution.py:25
  45.5 0.9 dynamic-slice_reduce_fusion.2
  46.5 6.1 %fusion.76 = bf16[16,512,256]{1,2,0:T(8,128)(2,1)} fusion(bf16[16,512,256]{1,2,0:T(8,128)(2,1)} %get-tuple-element.293, s32[]{:T(128)} %get-tuple-element.292, bf16[512,3584]{1,0:T(8,128)(2,1)} %get-tuple-element.308, s32[3584]{0:T(1024)S(1)} %get-tuple-element.267, s32[3584]{0:T(1024)S(1)} %get-tuple-element.268, ...), kind=kOutput, calls=%fused_computation.16.clone.1 | convolution fusion | flops 942800896 | bytes 4223492 | tf_op jit(solution)/shard_map/while/body/eval_jaxpr/dot_general | solution.py:25
  56.4 6.1 %fusion.76 = bf16[16,512,256]{1,2,0:T(8,128)(2,1)} fusion(bf16[16,512,256]{1,2,0:T(8,128)(2,1)} %get-tuple-element.293, s32[]{:T(128)} %get-tuple-element.292, bf16[512,3584]{1,0:T(8,128)(2,1)} %get-tuple-element.308, s32[3584]{0:T(1024)S(1)} %get-tuple-element.267, s32[3584]{0:T(1024)S(1)} %get-tuple-element.268, ...), kind=kOutput, calls=%fused_computation.16.clone.1 | convolution fusion | flops 942800896 | bytes 4223492 | tf_op jit(solution)/shard_map/while/body/eval_jaxpr/dot_general | solution.py:25
  66.3 6.1 %fusion.76 = bf16[16,512,256]{1,2,0:T(8,128)(2,1)} fusion(bf16[16,512,256]{1,2,0:T(8,128)(2,1)} %get-tuple-element.293, s32[]{:T(128)} %get-tuple-element.292, bf16[512,3584]{1,0:T(8,128)(2,1)} %get-tuple-element.308, s32[3584]{0:T(1024)S(1)} %get-tuple-element.267, s32[3584]{0:T(1024)S(1)} %get-tuple-element.268, ...), kind=kOutput, calls=%fused_computation.16.clone.1 | convolution fusion | flops 942800896 | bytes 4223492 | tf_op jit(solution)/shard_map/while/body/eval_jaxpr/dot_general | solution.py:25
  76.2 6.1 %fusion.76 = bf16[16,512,256]{1,2,0:T(8,128)(2,1)} fusion(bf16[16,512,256]{1,2,0:T(8,128)(2,1)} %get-tuple-element.293, s32[]{:T(128)} %get-tuple-element.292, bf16[512,3584]{1,0:T(8,128)(2,1)} %get-tuple-element.308, s32[3584]{0:T(1024)S(1)} %get-tuple-element.267, s32[3584]{0:T(1024)S(1)} %get-tuple-element.268, ...), kind=kOutput, calls=%fused_computation.16.clone.1 | convolution fusion | flops 942800896 | bytes 4223492 | tf_op jit(solution)/shard_map/while/body/eval_jaxpr/dot_general | solution.py:25
  86.1 6.1 %fusion.76 = bf16[16,512,256]{1,2,0:T(8,128)(2,1)} fusion(bf16[16,512,256]{1,2,0:T(8,128)(2,1)} %get-tuple-element.293, s32[]{:T(128)} %get-tuple-element.292, bf16[512,3584]{1,0:T(8,128)(2,1)} %get-tuple-element.308, s32[3584]{0:T(1024)S(1)} %get-tuple-element.267, s32[3584]{0:T(1024)S(1)} %get-tuple-element.268, ...), kind=kOutput, calls=%fused_computation.16.clone.1 | convolution fusion | flops 942800896 | bytes 4223492 | tf_op jit(solution)/shard_map/while/body/eval_jaxpr/dot_general | solution.py:25
  96.0 6.1 %fusion.76 = bf16[16,512,256]{1,2,0:T(8,128)(2,1)} fusion(bf16[16,512,256]{1,2,0:T(8,128)(2,1)} %get-tuple-element.293, s32[]{:T(128)} %get-tuple-element.292, bf16[512,3584]{1,0:T(8,128)(2,1)} %get-tuple-element.308, s32[3584]{0:T(1024)S(1)} %get-tuple-element.267, s32[3584]{0:T(1024)S(1)} %get-tuple-element.268, ...), kind=kOutput, calls=%fused_computation.16.clone.1 | convolution fusion | flops 942800896 | bytes 4223492 | tf_op jit(solution)/shard_map/while/body/eval_jaxpr/dot_general | solution.py:25
  105.9 6.1 %fusion.76 = bf16[16,512,256]{1,2,0:T(8,128)(2,1)} fusion(bf16[16,512,256]{1,2,0:T(8,128)(2,1)} %get-tuple-element.293, s32[]{:T(128)} %get-tuple-element.292, bf16[512,3584]{1,0:T(8,128)(2,1)} %get-tuple-element.308, s32[3584]{0:T(1024)S(1)} %get-tuple-element.267, s32[3584]{0:T(1024)S(1)} %get-tuple-element.268, ...), kind=kOutput, calls=%fused_computation.16.clone.1 | convolution fusion | flops 942800896 | bytes 4223492 | tf_op jit(solution)/shard_map/while/body/eval_jaxpr/dot_general | solution.py:25
  115.7 6.1 %fusion.76 = bf16[16,512,256]{1,2,0:T(8,128)(2,1)} fusion(bf16[16,512,256]{1,2,0:T(8,128)(2,1)} %get-tuple-element.293, s32[]{:T(128)} %get-tuple-element.292, bf16[512,3584]{1,0:T(8,128)(2,1)} %get-tuple-element.308, s32[3584]{0:T(1024)S(1)} %get-tuple-element.267, s32[3584]{0:T(1024)S(1)} %get-tuple-element.268, ...), kind=kOutput, calls=%fused_computation.16.clone.1 | convolution fusion | flops 942800896 | bytes 4223492 | tf_op jit(solution)/shard_map/while/body/eval_jaxpr/dot_general | solution.py:25
  125.6 6.1 %fusion.76 = bf16[16,512,256]{1,2,0:T(8,128)(2,1)} fusion(bf16[16,512,256]{1,2,0:T(8,128)(2,1)} %get-tuple-element.293, s32[]{:T(128)} %get-tuple-element.292, bf16[512,3584]{1,0:T(8,128)(2,1)} %get-tuple-element.308, s32[3584]{0:T(1024)S(1)} %get-tuple-element.267, s32[3584]{0:T(1024)S(1)} %get-tuple-element.268, ...), kind=kOutput, calls=%fused_computation.16.clone.1 | convolution fusion | flops 942800896 | bytes 4223492 | tf_op jit(solution)/shard_map/while/body/eval_jaxpr/dot_general | solution.py:25
  135.6 6.1 %fusion.76 = bf16[16,512,256]{1,2,0:T(8,128)(2,1)} fusion(bf16[16,512,256]{1,2,0:T(8,128)(2,1)} %get-tuple-element.293, s32[]{:T(128)} %get-tuple-element.292, bf16[512,3584]{1,0:T(8,128)(2,1)} %get-tuple-element.308, s32[3584]{0:T(1024)S(1)} %get-tuple-element.267, s32[3584]{0:T(1024)S(1)} %get-tuple-element.268, ...), kind=kOutput, calls=%fused_computation.16.clone.1 | convolution fusion | flops 942800896 | bytes 4223492 | tf_op jit(solution)/shard_map/while/body/eval_jaxpr/dot_general | solution.py:25
  144.5 0.9 dynamic-slice_reduce_fusion.2
  145.4 6.1 %fusion.76 = bf16[16,512,256]{1,2,0:T(8,128)(2,1)} fusion(bf16[16,512,256]{1,2,0:T(8,128)(2,1)} %get-tuple-element.293, s32[]{:T(128)} %get-tuple-element.292, bf16[512,3584]{1,0:T(8,128)(2,1)} %get-tuple-element.308, s32[3584]{0:T(1024)S(1)} %get-tuple-element.267, s32[3584]{0:T(1024)S(1)} %get-tuple-element.268, ...), kind=kOutput, calls=%fused_computation.16.clone.1 | convolution fusion | flops 942800896 | bytes 4223492 | tf_op jit(solution)/shard_map/while/body/eval_jaxpr/dot_general | solution.py:25
  155.3 6.1 %fusion.76 = bf16[16,512,256]{1,2,0:T(8,128)(2,1)} fusion(bf16[16,512,256]{1,2,0:T(8,128)(2,1)} %get-tuple-element.293, s32[]{:T(128)} %get-tuple-element.292, bf16[512,3584]{1,0:T(8,128)(2,1)} %get-tuple-element.308, s32[3584]{0:T(1024)S(1)} %get-tuple-element.267, s32[3584]{0:T(1024)S(1)} %get-tuple-element.268, ...), kind=kOutput, calls=%fused_computation.16.clone.1 | convolution fusion | flops 942800896 | bytes 4223492 | tf_op jit(solution)/shard_map/while/body/eval_jaxpr/dot_general | solution.py:25
  165.2 6.1 %fusion.76 = bf16[16,512,256]{1,2,0:T(8,128)(2,1)} fusion(bf16[16,512,256]{1,2,0:T(8,128)(2,1)} %get-tuple-element.293, s32[]{:T(128)} %get-tuple-element.292, bf16[512,3584]{1,0:T(8,128)(2,1)} %get-tuple-element.308, s32[3584]{0:T(1024)S(1)} %get-tuple-element.267, s32[3584]{0:T(1024)S(1)} %get-tuple-element.268, ...), kind=kOutput, calls=%fused_computation.16.clone.1 | convolution fusion | flops 942800896 | bytes 4223492 | tf_op jit(solution)/shard_map/while/body/eval_jaxpr/dot_general | solution.py:25
  171.3 4.6 convolution_bitcast_fusion
  176.0 6.7 %fusion.17 = f32[16,256,256]{1,2,0:T(8,128)} fusion(bf16[16,512,256]{1,2,0:T(8,128)(2,1)} %get-tuple-element.99, bf16[512]{0:T(512)(128)(2,1)S(1)} %convert_element_type.36), kind=kOutput, calls=%fused_computation.29 | convolution fusion | flops 1075838976 | bytes 8389632 | tf_op jit(solution)/shard_map/htk,htj->hkj/dot_general | solution.py:48
  183.4 24.0 %psum.14 = f32[]{:T(128)} all-reduce(f32[]{:T(128)} %convert_reduce_fusion), channel_id=1, replica_groups=mesh['seq'=8,'rep'=4] {'seq'}, use_global_device_ids=true, to_apply=%region_4.5 | all-reduce | flops 1 | bytes 8 | tf_op jit(solution)/shard_map/psum | solution.py:47
  208.0 34.9 %reduce-scatter.6.cloned.1.call-done = f32[2,64,256]{2,1,0:T(8,128)} async-done(((f32[16,64,256]{2,1,0:T(8,128)}), f32[2,64,256]{2,1,0:T(8,128)}) %reduce-scatter.6.cloned.1.call-update) | async-done | bytes 131088 | tf_op jit(solution)/shard_map/reduce_scatter | solution.py:63
  243.8 90.0 %reduce-scatter.4.cloned.1.call-done = f32[2,256,256]{1,2,0:T(8,128)} async-done(((f32[16,256,256]{1,2,0:T(8,128)}), f32[2,256,256]{1,2,0:T(8,128)}) %reduce-scatter.4.cloned.1.call-update) | async-done | bytes 524304 | tf_op jit(solution)/shard_map/reduce_scatter | solution.py:62
  333.8 1.1 select_add_fusion.1
  335.3 11.7 %cholesky.130 = f32[128,128]{1,0:T(8,128)S(1)} custom-call(f32[128,128]{1,0:T(8,128)S(1)} %cholesky.194), custom_call_target="Cholesky" | custom-call | tf_op jit(solution)/shard_map/jit(cholesky)/cholesky | solution.py:37
  347.0 9.8 %custom-call.15 = f32[1,128,128]{1,2,0:T(8,128)S(1)} custom-call(f32[1,128,128]{2,1,0:T(8,128)S(1)} %get-tuple-element.171), custom_call_target="InvertDiagBlocksLowerTriangular" | custom-call | tf_op jit(solution)/shard_map/jit(cholesky)/cholesky | solution.py:37
  357.3 11.7 %cholesky.147 = f32[128,128]{1,0:T(8,128)S(1)} custom-call(f32[128,128]{1,0:T(8,128)S(1)} %convolution_subtract_fusion.1), custom_call_target="Cholesky" | custom-call | tf_op jit(solution)/shard_map/jit(cholesky)/cholesky | solution.py:37
  371.7 3.7 while.18
  372.3 1.3 bitcast_dynamic-update-slice_fusion.4
  374.1 1.3 bitcast_dynamic-update-slice_fusion.4
  375.4 19.9 %custom-call.16 = f32[2,128,128]{1,2,0:T(8,128)S(1)} custom-call(f32[2,128,128]{2,1,0:T(8,128)S(1)} %get-tuple-element.128), custom_call_target="InvertDiagBlocksLowerTriangular" | custom-call | tf_op jit(solution)/shard_map/jit(_cho_solve)/triangular_solve | solution.py:38
  396.8 11.7 %cholesky.164 = f32[128,128]{1,0:T(8,128)S(1)} custom-call(f32[128,128]{1,0:T(8,128)S(1)} %cholesky.197), custom_call_target="Cholesky" | custom-call | tf_op jit(solution)/shard_map/jit(cholesky)/cholesky | solution.py:37
  408.6 9.8 %custom-call.17 = f32[1,128,128]{1,2,0:T(8,128)S(1)} custom-call(f32[1,128,128]{2,1,0:T(8,128)S(1)} %get-tuple-element.175), custom_call_target="InvertDiagBlocksLowerTriangular" | custom-call | tf_op jit(solution)/shard_map/jit(cholesky)/cholesky | solution.py:37
  418.9 11.7 %cholesky.181 = f32[128,128]{1,0:T(8,128)S(1)} custom-call(f32[128,128]{1,0:T(8,128)S(1)} %convolution_subtract_fusion), custom_call_target="Cholesky" | custom-call | tf_op jit(solution)/shard_map/jit(cholesky)/cholesky | solution.py:37
  433.3 4.1 while.19
  434.0 1.3 bitcast_dynamic-update-slice_fusion.5
  436.0 1.3 bitcast_dynamic-update-slice_fusion.5
  437.4 19.9 %custom-call.18 = f32[2,128,128]{1,2,0:T(8,128)S(1)} custom-call(f32[2,128,128]{2,1,0:T(8,128)S(1)} %get-tuple-element.129), custom_call_target="InvertDiagBlocksLowerTriangular" | custom-call | tf_op jit(solution)/shard_map/jit(_cho_solve)/triangular_solve | solution.py:38
  458.8 31.4 %all_gather.3 = bf16[16,256,64]{1,2,0:T(8,128)(2,1)S(1)} all-gather(bf16[2,256,64]{1,2,0:T(8,128)(2,1)S(1)} %pad_maximum_fusion), channel_id=1, replica_groups=mesh['seq'=8,'rep'=4] {'seq'}, dimensions={0}, use_global_device_ids=true | all-gather | bytes 589824 | tf_op jit(solution)/shard_map/all_gather | solution.py:71
  490.2 3.7 convolution_bitcast_fusion.1
  494.0 19.3 %reduce-scatter.8.cloned.1.call-done = f32[128,64]{0,1:T(8,128)} async-done(((f32[512,64]{0,1:T(8,128)}), f32[128,64]{0,1:T(8,128)}) %reduce-scatter.8.cloned.1.call-update) | async-done | bytes 32784 | tf_op jit(solution)/shard_map/reduce_scatter | solution.py:73
  514.1 39.3 %psum.15 = f32[64]{0:T(128)S(1)} all-reduce(f32[64]{0:T(128)S(1)} %fusion.45), channel_id=1, replica_groups=mesh['seq'=8,'rep'=4] {'seq','rep'}, use_global_device_ids=true, to_apply=%region_12.15 | all-reduce | flops 64 | bytes 512 | tf_op jit(solution)/shard_map/psum | solution.py:77
  553.4 1.5 broadcast_divide_fusion
  (110 shorter events, 31.8 us)
Async XLA Ops:
  6.5 236.4 %reduce-scatter.6.cloned.1.call-start = ((), (), s32[]{:S(2)}) async-start(), calls=%async_computation.4 | async-start | bytes 1179648 | tf_op jit(solution)/shard_map/reduce_scatter | solution.py:63
  13.0 158.3 %copy-start.1 = (s32[64]{0:T(128)S(1)}, s32[64]{0:T(128)}, u32[]{:S(2)}) copy-start(s32[64]{0:T(128)} %param.14) | copy-start | bytes 772
  171.3 4.7 copy-start
  176.0 157.9 %reduce-scatter.4.cloned.1.call-start = ((), (), s32[]{:S(2)}) async-start(), calls=%async_computation.3 | async-start | bytes 4718592 | tf_op jit(solution)/shard_map/reduce_scatter | solution.py:62
  182.8 330.5 %reduce-scatter.8.cloned.1.call-start = ((), (), s32[]{:S(2)}) async-start(), calls=%async_computation.5 | async-start | bytes 163840 | tf_op jit(solution)/shard_map/reduce_scatter | solution.py:73
Sparse Core Ops, SparseCore 0:
  176.1 66.8 reduce-scatter.5
  246.6 87.2 reduce-scatter.3
  494.0 19.2 reduce-scatter.7
where the time goes:
time: 564 us; the launch traced here: 561 us
  waiting for transfers between devices  144 us (26%)
  matrix products  116 us (21%)
  other arithmetic  114 us (20%)
  blocking collectives  94.6 us (17%)
  local copies, waits for them, and re-layouts  39.5 us (7%)
  loops' own time  36.8 us (7%)
  between operations  16.5 us (3%)
    dot_general x16, matrix products, one_head(): counted = jnp.dot(gradient, count_table, preferred_element_type=jnp.float32)  97.2 us
    reduce_scatter x1, waiting for transfers between devices, on_device(): lax.psum_scatter(local_grams, 'seq', scatter_dimension=0, tiled=True)  90 us
    another operation x14, other arithmetic, solve_queries(): factor = jnp.linalg.cholesky(gram_sum)  69.2 us
    another operation x5, other arithmetic, solve_queries(): jax.scipy.linalg.cho_solve((factor, True), chosen.T).astype(jnp.bfloat16)  39.9 us
    psum x1, blocking collectives, on_device(): norm_sum = lax.psum(partial_value, ('seq', 'rep')) / token_count  39.3 us
    another operation x1, loops' own time, build_sketches(): return lax.map(one_head, jnp.arange(head_count, dtype=jnp.int32))  36.7 us
    reduce_scatter x1, waiting for transfers between devices, on_device(): lax.psum_scatter(local_chosen, 'seq', scatter_dimension=0, tiled=True)  34.9 us
    all_gather x1, blocking collectives, on_device(): solved_all = lax.all_gather(solved, 'seq', axis=0, tiled=True)  31.4 us
  transfers between devices with their start and end apart: 3, of which 3 were waited for; matrix products, arithmetic and copies ran while one was open for 1% of the time, Pallas kernels for 0%

commit v1 on v0

--- a/solution.py
+++ b/solution.py
@@ -74,7 +74,7 @@
     row_start = lax.axis_index("rep") * out_rows
     mask_rows = lax.dynamic_slice_in_dim(loss_mask, row_start, out_rows, 0).astype(jnp.float32)
     partial_value = jnp.sum(mask_rows[:, None] * contrib * contrib, 0)
-    norm_sum = lax.psum(partial_value, ("seq", "rep")) / token_count
+    norm_sum = jnp.sum(lax.all_gather(partial_value, ("seq", "rep")), axis=0) / token_count
     return contrib / jnp.sqrt(norm_sum + norm_floor)
 
 

time: 564 us -> 564 us (level)
    unnamed x0 -> x1, blocking collectives: none -> 39.3 us
    psum x1 -> x0, blocking collectives: 39.3 us -> none  [on_device(): norm_sum = lax.psum(partial_value, ('seq', 'rep')) / token_count]
where the time goes in v1:
time: 564 us; the launch traced here: 562 us
  waiting for transfers between devices  144 us (26%)
  matrix products  116 us (21%)
  other arithmetic  114 us (20%)
  blocking collectives  94.6 us (17%)
  local copies, waits for them, and re-layouts  39.9 us (7%)
  loops' own time  36.8 us (7%)
  between operations  16.5 us (3%)
    dot_general x16, matrix products, one_head(): counted = jnp.dot(gradient, count_table, preferred_element_type=jnp.float32)  97.2 us
    reduce_scatter x1, waiting for transfers between devices, on_device(): lax.psum_scatter(local_grams, 'seq', scatter_dimension=0, tiled=True)  90 us
    another operation x14, other arithmetic, solve_queries(): factor = jnp.linalg.cholesky(gram_sum)  69.2 us
    another operation x5, other arithmetic, solve_queries(): jax.scipy.linalg.cho_solve((factor, True), chosen.T).astype(jnp.bfloat16)  39.9 us
    unnamed x1, blocking collectives  39.3 us
    another operation x1, loops' own time, build_sketches(): return lax.map(one_head, jnp.arange(head_count, dtype=jnp.int32))  36.7 us
    reduce_scatter x1, waiting for transfers between devices, on_device(): lax.psum_scatter(local_chosen, 'seq', scatter_dimension=0, tiled=True)  34.9 us
    all_gather x1, blocking collectives, on_device(): solved_all = lax.all_gather(solved, 'seq', axis=0, tiled=True)  31.4 us
  transfers between devices with their start and end apart: 3, of which 3 were waited for; matrix products, arithmetic and copies ran while one was open for 1% of the time, Pallas kernels for 0%

profile of v1, /device:TPU:0, one launch (start us, length us, event | category | flops | bytes accessed | tf_op | source)
XLA Modules:
  0.0 561.5 jit_solution(14013833207641903197)
XLA Ops:
  6.5 6.5 %copy.20 = bf16[1,512,4096]{1,2,0:T(8,128)(2,1)} copy(bf16[1,512,4096]{2,1,0:T(8,128)(2,1)} %param.10) | data formatting | bytes 8388608 | tf_op args[0]
  13.0 158.3 %while.17 = (s32[]{:T(128)}, bf16[16,512,256]{1,2,0:T(8,128)(2,1)}, s32[16]{0:T(128)S(1)}, bf16[512,4096]{0,1:T(8,128)(2,1)}, s32[16,3584]{1,0:T(8,128)}, /*inde...) while((s32[]{:T(128)}, bf16[16,512,256]{1,2,0:T(8,128)(2,1)}, ...), condition=%wide.region_1.2_spmd.clone, body=%wide.region_0.1_spmd.clone.sunk | while | flops 942876160 | bytes 4295377 | solution.py:31
  15.8 0.9 dynamic-slice_reduce_fusion.2
  16.8 6.1 %fusion.76 = bf16[16,512,256]{1,2,0:T(8,128)(2,1)} fusion(bf16[16,512,256]{1,2,0:T(8,128)(2,1)} %get-tuple-element.293, s32[]{:T(128)} %get-tuple-element.292, bf16[512,3584]{1,0:T(8,128)(2,1)} %get-tuple-element.308, s32[3584]{0:T(1024)S(1)} %get-tuple-element.267, s32[3584]{0:T(1024)S(1)} %get-tuple-element.268, ...), kind=kOutput, calls=%fused_computation.16.clone.1 | convolution fusion | flops 942800896 | bytes 4223492 | tf_op jit(solution)/shard_map/while/body/eval_jaxpr/dot_general | solution.py:25
  25.7 0.9 dynamic-slice_reduce_fusion.2
  26.7 6.1 %fusion.76 = bf16[16,512,256]{1,2,0:T(8,128)(2,1)} fusion(bf16[16,512,256]{1,2,0:T(8,128)(2,1)} %get-tuple-element.293, s32[]{:T(128)} %get-tuple-element.292, bf16[512,3584]{1,0:T(8,128)(2,1)} %get-tuple-element.308, s32[3584]{0:T(1024)S(1)} %get-tuple-element.267, s32[3584]{0:T(1024)S(1)} %get-tuple-element.268, ...), kind=kOutput, calls=%fused_computation.16.clone.1 | convolution fusion | flops 942800896 | bytes 4223492 | tf_op jit(solution)/shard_map/while/body/eval_jaxpr/dot_general | solution.py:25
  35.6 0.9 dynamic-slice_reduce_fusion.2
  36.6 6.1 %fusion.76 = bf16[16,512,256]{1,2,0:T(8,128)(2,1)} fusion(bf16[16,512,256]{1,2,0:T(8,128)(2,1)} %get-tuple-element.293, s32[]{:T(128)} %get-tuple-element.292, bf16[512,3584]{1,0:T(8,128)(2,1)} %get-tuple-element.308, s32[3584]{0:T(1024)S(1)} %get-tuple-element.267, s32[3584]{0:T(1024)S(1)} %get-tuple-element.268, ...), kind=kOutput, calls=%fused_computation.16.clone.1 | convolution fusion | flops 942800896 | bytes 4223492 | tf_op jit(solution)/shard_map/while/body/eval_jaxpr/dot_general | solution.py:25
  45.5 0.9 dynamic-slice_reduce_fusion.2
  46.5 6.1 %fusion.76 = bf16[16,512,256]{1,2,0:T(8,128)(2,1)} fusion(bf16[16,512,256]{1,2,0:T(8,128)(2,1)} %get-tuple-element.293, s32[]{:T(128)} %get-tuple-element.292, bf16[512,3584]{1,0:T(8,128)(2,1)} %get-tuple-element.308, s32[3584]{0:T(1024)S(1)} %get-tuple-element.267, s32[3584]{0:T(1024)S(1)} %get-tuple-element.268, ...), kind=kOutput, calls=%fused_computation.16.clone.1 | convolution fusion | flops 942800896 | bytes 4223492 | tf_op jit(solution)/shard_map/while/body/eval_jaxpr/dot_general | solution.py:25
  56.4 6.1 %fusion.76 = bf16[16,512,256]{1,2,0:T(8,128)(2,1)} fusion(bf16[16,512,256]{1,2,0:T(8,128)(2,1)} %get-tuple-element.293, s32[]{:T(128)} %get-tuple-element.292, bf16[512,3584]{1,0:T(8,128)(2,1)} %get-tuple-element.308, s32[3584]{0:T(1024)S(1)} %get-tuple-element.267, s32[3584]{0:T(1024)S(1)} %get-tuple-element.268, ...), kind=kOutput, calls=%fused_computation.16.clone.1 | convolution fusion | flops 942800896 | bytes 4223492 | tf_op jit(solution)/shard_map/while/body/eval_jaxpr/dot_general | solution.py:25
  66.3 6.1 %fusion.76 = bf16[16,512,256]{1,2,0:T(8,128)(2,1)} fusion(bf16[16,512,256]{1,2,0:T(8,128)(2,1)} %get-tuple-element.293, s32[]{:T(128)} %get-tuple-element.292, bf16[512,3584]{1,0:T(8,128)(2,1)} %get-tuple-element.308, s32[3584]{0:T(1024)S(1)} %get-tuple-element.267, s32[3584]{0:T(1024)S(1)} %get-tuple-element.268, ...), kind=kOutput, calls=%fused_computation.16.clone.1 | convolution fusion | flops 942800896 | bytes 4223492 | tf_op jit(solution)/shard_map/while/body/eval_jaxpr/dot_general | solution.py:25
  76.2 6.1 %fusion.76 = bf16[16,512,256]{1,2,0:T(8,128)(2,1)} fusion(bf16[16,512,256]{1,2,0:T(8,128)(2,1)} %get-tuple-element.293, s32[]{:T(128)} %get-tuple-element.292, bf16[512,3584]{1,0:T(8,128)(2,1)} %get-tuple-element.308, s32[3584]{0:T(1024)S(1)} %get-tuple-element.267, s32[3584]{0:T(1024)S(1)} %get-tuple-element.268, ...), kind=kOutput, calls=%fused_computation.16.clone.1 | convolution fusion | flops 942800896 | bytes 4223492 | tf_op jit(solution)/shard_map/while/body/eval_jaxpr/dot_general | solution.py:25
  86.1 6.1 %fusion.76 = bf16[16,512,256]{1,2,0:T(8,128)(2,1)} fusion(bf16[16,512,256]{1,2,0:T(8,128)(2,1)} %get-tuple-element.293, s32[]{:T(128)} %get-tuple-element.292, bf16[512,3584]{1,0:T(8,128)(2,1)} %get-tuple-element.308, s32[3584]{0:T(1024)S(1)} %get-tuple-element.267, s32[3584]{0:T(1024)S(1)} %get-tuple-element.268, ...), kind=kOutput, calls=%fused_computation.16.clone.1 | convolution fusion | flops 942800896 | bytes 4223492 | tf_op jit(solution)/shard_map/while/body/eval_jaxpr/dot_general | solution.py:25
  96.0 6.1 %fusion.76 = bf16[16,512,256]{1,2,0:T(8,128)(2,1)} fusion(bf16[16,512,256]{1,2,0:T(8,128)(2,1)} %get-tuple-element.293, s32[]{:T(128)} %get-tuple-element.292, bf16[512,3584]{1,0:T(8,128)(2,1)} %get-tuple-element.308, s32[3584]{0:T(1024)S(1)} %get-tuple-element.267, s32[3584]{0:T(1024)S(1)} %get-tuple-element.268, ...), kind=kOutput, calls=%fused_computation.16.clone.1 | convolution fusion | flops 942800896 | bytes 4223492 | tf_op jit(solution)/shard_map/while/body/eval_jaxpr/dot_general | solution.py:25
  105.9 6.1 %fusion.76 = bf16[16,512,256]{1,2,0:T(8,128)(2,1)} fusion(bf16[16,512,256]{1,2,0:T(8,128)(2,1)} %get-tuple-element.293, s32[]{:T(128)} %get-tuple-element.292, bf16[512,3584]{1,0:T(8,128)(2,1)} %get-tuple-element.308, s32[3584]{0:T(1024)S(1)} %get-tuple-element.267, s32[3584]{0:T(1024)S(1)} %get-tuple-element.268, ...), kind=kOutput, calls=%fused_computation.16.clone.1 | convolution fusion | flops 942800896 | bytes 4223492 | tf_op jit(solution)/shard_map/while/body/eval_jaxpr/dot_general | solution.py:25
  115.7 6.1 %fusion.76 = bf16[16,512,256]{1,2,0:T(8,128)(2,1)} fusion(bf16[16,512,256]{1,2,0:T(8,128)(2,1)} %get-tuple-element.293, s32[]{:T(128)} %get-tuple-element.292, bf16[512,3584]{1,0:T(8,128)(2,1)} %get-tuple-element.308, s32[3584]{0:T(1024)S(1)} %get-tuple-element.267, s32[3584]{0:T(1024)S(1)} %get-tuple-element.268, ...), kind=kOutput, calls=%fused_computation.16.clone.1 | convolution fusion | flops 942800896 | bytes 4223492 | tf_op jit(solution)/shard_map/while/body/eval_jaxpr/dot_general | solution.py:25
  125.6 6.1 %fusion.76 = bf16[16,512,256]{1,2,0:T(8,128)(2,1)} fusion(bf16[16,512,256]{1,2,0:T(8,128)(2,1)} %get-tuple-element.293, s32[]{:T(128)} %get-tuple-element.292, bf16[512,3584]{1,0:T(8,128)(2,1)} %get-tuple-element.308, s32[3584]{0:T(1024)S(1)} %get-tuple-element.267, s32[3584]{0:T(1024)S(1)} %get-tuple-element.268, ...), kind=kOutput, calls=%fused_computation.16.clone.1 | convolution fusion | flops 942800896 | bytes 4223492 | tf_op jit(solution)/shard_map/while/body/eval_jaxpr/dot_general | solution.py:25
  135.6 6.1 %fusion.76 = bf16[16,512,256]{1,2,0:T(8,128)(2,1)} fusion(bf16[16,512,256]{1,2,0:T(8,128)(2,1)} %get-tuple-element.293, s32[]{:T(128)} %get-tuple-element.292, bf16[512,3584]{1,0:T(8,128)(2,1)} %get-tuple-element.308, s32[3584]{0:T(1024)S(1)} %get-tuple-element.267, s32[3584]{0:T(1024)S(1)} %get-tuple-element.268, ...), kind=kOutput, calls=%fused_computation.16.clone.1 | convolution fusion | flops 942800896 | bytes 4223492 | tf_op jit(solution)/shard_map/while/body/eval_jaxpr/dot_general | solution.py:25
  144.5 0.9 dynamic-slice_reduce_fusion.2
  145.4 6.1 %fusion.76 = bf16[16,512,256]{1,2,0:T(8,128)(2,1)} fusion(bf16[16,512,256]{1,2,0:T(8,128)(2,1)} %get-tuple-element.293, s32[]{:T(128)} %get-tuple-element.292, bf16[512,3584]{1,0:T(8,128)(2,1)} %get-tuple-element.308, s32[3584]{0:T(1024)S(1)} %get-tuple-element.267, s32[3584]{0:T(1024)S(1)} %get-tuple-element.268, ...), kind=kOutput, calls=%fused_computation.16.clone.1 | convolution fusion | flops 942800896 | bytes 4223492 | tf_op jit(solution)/shard_map/while/body/eval_jaxpr/dot_general | solution.py:25
  155.3 6.1 %fusion.76 = bf16[16,512,256]{1,2,0:T(8,128)(2,1)} fusion(bf16[16,512,256]{1,2,0:T(8,128)(2,1)} %get-tuple-element.293, s32[]{:T(128)} %get-tuple-element.292, bf16[512,3584]{1,0:T(8,128)(2,1)} %get-tuple-element.308, s32[3584]{0:T(1024)S(1)} %get-tuple-element.267, s32[3584]{0:T(1024)S(1)} %get-tuple-element.268, ...), kind=kOutput, calls=%fused_computation.16.clone.1 | convolution fusion | flops 942800896 | bytes 4223492 | tf_op jit(solution)/shard_map/while/body/eval_jaxpr/dot_general | solution.py:25
  165.2 6.1 %fusion.76 = bf16[16,512,256]{1,2,0:T(8,128)(2,1)} fusion(bf16[16,512,256]{1,2,0:T(8,128)(2,1)} %get-tuple-element.293, s32[]{:T(128)} %get-tuple-element.292, bf16[512,3584]{1,0:T(8,128)(2,1)} %get-tuple-element.308, s32[3584]{0:T(1024)S(1)} %get-tuple-element.267, s32[3584]{0:T(1024)S(1)} %get-tuple-element.268, ...), kind=kOutput, calls=%fused_computation.16.clone.1 | convolution fusion | flops 942800896 | bytes 4223492 | tf_op jit(solution)/shard_map/while/body/eval_jaxpr/dot_general | solution.py:25
  171.3 4.6 convolution_bitcast_fusion
  176.0 6.7 %fusion.17 = f32[16,256,256]{1,2,0:T(8,128)} fusion(bf16[16,512,256]{1,2,0:T(8,128)(2,1)} %get-tuple-element.99, bf16[512]{0:T(512)(128)(2,1)S(1)} %convert_element_type.36), kind=kOutput, calls=%fused_computation.29 | convolution fusion | flops 1075838976 | bytes 8389632 | tf_op jit(solution)/shard_map/htk,htj->hkj/dot_general | solution.py:48
  183.4 24.0 %psum.7 = f32[]{:T(128)} all-reduce(f32[]{:T(128)} %convert_reduce_fusion), channel_id=1, replica_groups=mesh['seq'=8,'rep'=4] {'seq'}, use_global_device_ids=true, to_apply=%region_4.5 | all-reduce | flops 1 | bytes 8 | tf_op jit(solution)/shard_map/psum | solution.py:47
  208.0 34.9 %reduce-scatter.6.cloned.1.call-done = f32[2,64,256]{2,1,0:T(8,128)} async-done(((f32[16,64,256]{2,1,0:T(8,128)}), f32[2,64,256]{2,1,0:T(8,128)}) %reduce-scatter.6.cloned.1.call-update) | async-done | bytes 131088 | tf_op jit(solution)/shard_map/reduce_scatter | solution.py:63
  243.8 90.0 %reduce-scatter.4.cloned.1.call-done = f32[2,256,256]{1,2,0:T(8,128)} async-done(((f32[16,256,256]{1,2,0:T(8,128)}), f32[2,256,256]{1,2,0:T(8,128)}) %reduce-scatter.4.cloned.1.call-update) | async-done | bytes 524304 | tf_op jit(solution)/shard_map/reduce_scatter | solution.py:62
  333.8 1.1 select_add_fusion.1
  335.3 11.7 %cholesky.130 = f32[128,128]{1,0:T(8,128)S(1)} custom-call(f32[128,128]{1,0:T(8,128)S(1)} %cholesky.194), custom_call_target="Cholesky" | custom-call | tf_op jit(solution)/shard_map/jit(cholesky)/cholesky | solution.py:37
  347.0 9.8 %custom-call.15 = f32[1,128,128]{1,2,0:T(8,128)S(1)} custom-call(f32[1,128,128]{2,1,0:T(8,128)S(1)} %get-tuple-element.171), custom_call_target="InvertDiagBlocksLowerTriangular" | custom-call | tf_op jit(solution)/shard_map/jit(cholesky)/cholesky | solution.py:37
  357.3 11.7 %cholesky.147 = f32[128,128]{1,0:T(8,128)S(1)} custom-call(f32[128,128]{1,0:T(8,128)S(1)} %convolution_subtract_fusion.1), custom_call_target="Cholesky" | custom-call | tf_op jit(solution)/shard_map/jit(cholesky)/cholesky | solution.py:37
  371.7 3.7 while.18
  372.3 1.3 bitcast_dynamic-update-slice_fusion.4
  374.1 1.3 bitcast_dynamic-update-slice_fusion.4
  375.4 19.9 %custom-call.16 = f32[2,128,128]{1,2,0:T(8,128)S(1)} custom-call(f32[2,128,128]{2,1,0:T(8,128)S(1)} %get-tuple-element.128), custom_call_target="InvertDiagBlocksLowerTriangular" | custom-call | tf_op jit(solution)/shard_map/jit(_cho_solve)/triangular_solve | solution.py:38
  396.7 11.7 %cholesky.164 = f32[128,128]{1,0:T(8,128)S(1)} custom-call(f32[128,128]{1,0:T(8,128)S(1)} %cholesky.197), custom_call_target="Cholesky" | custom-call | tf_op jit(solution)/shard_map/jit(cholesky)/cholesky | solution.py:37
  408.4 9.8 %custom-call.17 = f32[1,128,128]{1,2,0:T(8,128)S(1)} custom-call(f32[1,128,128]{2,1,0:T(8,128)S(1)} %get-tuple-element.175), custom_call_target="InvertDiagBlocksLowerTriangular" | custom-call | tf_op jit(solution)/shard_map/jit(cholesky)/cholesky | solution.py:37
  418.8 11.7 %cholesky.181 = f32[128,128]{1,0:T(8,128)S(1)} custom-call(f32[128,128]{1,0:T(8,128)S(1)} %convolution_subtract_fusion), custom_call_target="Cholesky" | custom-call | tf_op jit(solution)/shard_map/jit(cholesky)/cholesky | solution.py:37
  433.2 4.1 while.19
  433.9 1.3 bitcast_dynamic-update-slice_fusion.5
  435.9 1.3 bitcast_dynamic-update-slice_fusion.5
  437.3 19.9 %custom-call.18 = f32[2,128,128]{1,2,0:T(8,128)S(1)} custom-call(f32[2,128,128]{2,1,0:T(8,128)S(1)} %get-tuple-element.129), custom_call_target="InvertDiagBlocksLowerTriangular" | custom-call | tf_op jit(solution)/shard_map/jit(_cho_solve)/triangular_solve | solution.py:38
  458.5 31.4 %all_gather.9 = bf16[16,256,64]{1,2,0:T(8,128)(2,1)S(1)} all-gather(bf16[2,256,64]{1,2,0:T(8,128)(2,1)S(1)} %pad_maximum_fusion), channel_id=1, replica_groups=mesh['seq'=8,'rep'=4] {'seq'}, dimensions={0}, use_global_device_ids=true | all-gather | bytes 589824 | tf_op jit(solution)/shard_map/all_gather | solution.py:71
  489.9 3.7 convolution_bitcast_fusion.1
  493.7 19.3 %reduce-scatter.8.cloned.1.call-done = f32[128,64]{0,1:T(8,128)} async-done(((f32[512,64]{0,1:T(8,128)}), f32[128,64]{0,1:T(8,128)}) %reduce-scatter.8.cloned.1.call-update) | async-done | bytes 32784 | tf_op jit(solution)/shard_map/reduce_scatter | solution.py:73
  514.1 39.3 %all-reduce.1 = f32[2048]{0:T(1024)S(1)} all-reduce(f32[2048]{0:T(1024)S(1)} %dynamic-update-slice.9), channel_id=2, replica_groups=mesh['seq'=8,'rep'=4] {'seq','rep'}, use_global_device_ids=true, to_apply=%add.1 | all-reduce | flops 2048 | bytes 16384
  553.5 1.5 broadcast_divide_fusion
  (114 shorter events, 31.9 us)
Async XLA Ops:
  6.5 236.4 %reduce-scatter.6.cloned.1.call-start = ((), (), s32[]{:S(2)}) async-start(), calls=%async_computation.4 | async-start | bytes 1179648 | tf_op jit(solution)/shard_map/reduce_scatter | solution.py:63
  13.0 158.3 %copy-start.1 = (s32[64]{0:T(128)S(1)}, s32[64]{0:T(128)}, u32[]{:S(2)}) copy-start(s32[64]{0:T(128)} %param.14) | copy-start | bytes 772
  171.3 4.7 copy-start
  176.0 157.9 %reduce-scatter.4.cloned.1.call-start = ((), (), s32[]{:S(2)}) async-start(), calls=%async_computation.3 | async-start | bytes 4718592 | tf_op jit(solution)/shard_map/reduce_scatter | solution.py:62
  182.8 330.2 %reduce-scatter.8.cloned.1.call-start = ((), (), s32[]{:S(2)}) async-start(), calls=%async_computation.5 | async-start | bytes 163840 | tf_op jit(solution)/shard_map/reduce_scatter | solution.py:73
Sparse Core Ops, SparseCore 0:
  176.1 66.8 reduce-scatter.5
  246.6 87.2 reduce-scatter.3
  493.7 19.1 reduce-scatter.7
